TPU v7x, 256 devices: a whole 4x4x8 slice. The times are simulated.
256 devices in a mesh: batch: 4 (over x_lo, core), seq: 64 (over y, x_hi, z).
Axes of the slice: x: 4 (x_hi: 2, x_lo: 2; x = x_hi * 2 + x_lo), y: 4, z: 8, core: 2. Of those that a mesh axis runs over, the one named last changes fastest.
Arguments:
- signal: bfloat16 [4, 16384, 256], P('batch', 'seq'), may hold values from -0.125 to 0.125
- grad_out: bfloat16 [4, 16384, 256], P('batch', 'seq'), may hold values from -6 to 6
- filter_taps: float32 [16384, 256], P('seq'), may hold values from -0.125 to 0.125
- skip_gain: float32 [256], replicated, may hold values from 0.5 to 2
Outputs:
- input_grad: bfloat16 [4, 16384, 256], P('batch', 'seq')
- filter_grad: float32 [16384, 256], P('seq')
All inputs are finite; a program needn't handle non-finite values.
Results may differ from a plain program's by a relative error of at most 0.001.
Values sent between devices are 32-bit elements; how exact they have to be, the bound alone decides.
A program may use at most 64 MiB of HBM per device.

v0:
```python
import jax
import jax.numpy as jnp
from jax import lax
from jax.sharding import PartitionSpec as P


def split_up(x, dim, devices):
    shape = x.shape
    parts = x.reshape(*shape[:dim], devices, shape[dim] // devices, *shape[dim + 1 :])
    return jnp.moveaxis(parts, dim, 0)


def summed_on_arrival(x, axis, dim):
    parts = split_up(x, dim, lax.axis_size(axis))
    arrived = lax.all_to_all(parts, axis, split_axis=0, concat_axis=0, tiled=True)
    return arrived.sum(axis=0)


def copy_for_each(x, axis):
    devices = lax.axis_size(axis)
    return lax.all_to_all(jnp.broadcast_to(x[None], (devices, *x.shape)), axis, 0, 0, tiled=True)


def in_order(parts, dim):
    shape = list(parts.shape[1:])
    shape[dim] *= parts.shape[0]
    return jnp.moveaxis(parts, 0, dim).reshape(shape)


def gather_directly(x, axis, dim):
    parts = copy_for_each(x, axis)
    return in_order(parts, dim)


def angle_table(height, width, period):
    product = lax.broadcasted_iota(jnp.int32, (height, width), 0) * lax.broadcasted_iota(
        jnp.int32, (height, width), 1
    )
    return 2.0 * jnp.pi / period * (product % period).astype(jnp.float32)


def angle_of(product, period):
    return 2.0 * jnp.pi / period * (product % period).astype(jnp.float32)


def coarse_order(slot, seq_count):
    pair_index = slot // 2
    odd_slot = slot % 2
    return jnp.where(
        pair_index == 0,
        odd_slot * seq_count,
        jnp.where(odd_slot == 0, pair_index, 2 * seq_count - pair_index),
    )


def contract(form, table, operand):
    return jnp.einsum(form, table, operand, precision=lax.Precision.HIGHEST)


def forward_spectra(columns):
    seq_count = lax.axis_size("seq")
    row_count = columns.shape[0]
    part_rows = row_count // seq_count
    period_len = 2 * row_count * seq_count
    spread = lax.all_to_all(
        columns.reshape(1, row_count, columns.shape[1]),
        "seq",
        split_axis=1,
        concat_axis=0,
        tiled=True,
    )
    slot_grid = lax.broadcasted_iota(jnp.int32, (2 * seq_count, seq_count), 0)
    source_grid = lax.broadcasted_iota(jnp.int32, (2 * seq_count, seq_count), 1)
    first_table = angle_of(coarse_order(slot_grid, seq_count) * source_grid, 2 * seq_count)
    cos_first = jnp.cos(first_table)
    sin_first = jnp.sin(first_table)
    half_width = spread.shape[2] // 2
    real_in = spread[:, :, :half_width]
    imag_in = spread[:, :, half_width:]
    real_part = contract("ks,srw->krw", cos_first, real_in) + contract(
        "ks,srw->krw", sin_first, imag_in
    )
    imag_part = contract("ks,srw->krw", cos_first, imag_in) - contract(
        "ks,srw->krw", sin_first, real_in
    )
    global_row = lax.axis_index("seq") * part_rows + lax.broadcasted_iota(
        jnp.int32, (2 * seq_count, part_rows), 1
    )
    coarse = coarse_order(lax.broadcasted_iota(jnp.int32, (2 * seq_count, part_rows), 0), seq_count)
    phases = angle_of(global_row * coarse, period_len)
    cos_turn = jnp.cos(phases)[:, :, None]
    sin_turn = jnp.sin(phases)[:, :, None]
    rotated = jnp.stack(
        [real_part * cos_turn + imag_part * sin_turn, imag_part * cos_turn - real_part * sin_turn]
    )
    inner_table = angle_table(row_count, row_count, row_count)
    cos_inner = jnp.cos(inner_table)
    sin_inner = jnp.sin(inner_table)
    pieces = lax.all_to_all(rotated, "seq", split_axis=1, concat_axis=2, tiled=True)
    real_sum = contract("qr,krw->kqw", cos_inner, pieces[0]) + contract(
        "qr,krw->kqw", sin_inner, pieces[1]
    )
    imag_sum = contract("qr,krw->kqw", cos_inner, pieces[1]) - contract(
        "qr,krw->kqw", sin_inner, pieces[0]
    )
    return jnp.stack([real_sum, imag_sum])


def split_pairs(packed):
    reversed_q = packed[:, :, ::-1]
    zero_row = jnp.roll(reversed_q[:, 0], 1, axis=1)
    own_pair = jnp.stack([zero_row, reversed_q[:, 1]], axis=1)
    partner = jnp.where(lax.axis_index("seq") == 0, own_pair, reversed_q[:, ::-1])
    first = jnp.stack([0.5 * (packed[0] + partner[0]), 0.5 * (packed[1] - partner[1])])
    second = jnp.stack([0.5 * (packed[1] + partner[1]), 0.5 * (partner[0] - packed[0])])
    return (first, second)


def inverse_rows(spectra):
    seq_count = lax.axis_size("seq")
    row_count = spectra.shape[2]
    period_len = 2 * row_count * seq_count
    inner_table = angle_table(row_count, row_count, row_count)
    cos_inner = jnp.cos(inner_table)
    sin_inner = jnp.sin(inner_table)
    real_sum = contract("qr,krw->kqw", cos_inner, spectra[0]) - contract(
        "qr,krw->kqw", sin_inner, spectra[1]
    )
    imag_sum = contract("qr,krw->kqw", cos_inner, spectra[1]) + contract(
        "qr,krw->kqw", sin_inner, spectra[0]
    )
    coarse = coarse_order(
        2 * lax.axis_index("seq") + lax.broadcasted_iota(jnp.int32, (2, row_count), 0), seq_count
    )
    position = lax.broadcasted_iota(jnp.int32, (2, row_count), 1)
    phases = angle_of(position * coarse, period_len)
    cos_turn = jnp.cos(phases)[:, :, None]
    sin_turn = jnp.sin(phases)[:, :, None]
    rotated = jnp.stack(
        [real_sum * cos_turn - imag_sum * sin_turn, real_sum * sin_turn + imag_sum * cos_turn]
    )
    target_grid = lax.broadcasted_iota(jnp.int32, (seq_count, 2 * seq_count), 0)
    slot_grid = lax.broadcasted_iota(jnp.int32, (seq_count, 2 * seq_count), 1)
    last_table = angle_of(target_grid * coarse_order(slot_grid, seq_count), 2 * seq_count)
    cos_last = jnp.cos(last_table)
    sin_last = jnp.sin(last_table)
    pieces = lax.all_to_all(rotated, "seq", split_axis=2, concat_axis=1, tiled=True)
    value = contract("sk,krw->srw", cos_last, pieces[0]) - contract(
        "sk,krw->srw", sin_last, pieces[1]
    )
    other = contract("sk,krw->srw", sin_last, pieces[0]) + contract(
        "sk,krw->srw", cos_last, pieces[1]
    )
    gathered = (value / period_len, other / period_len)
    gathered = jnp.concatenate([gathered[0], gathered[1]], axis=2)
    home_rows = lax.all_to_all(gathered, "seq", split_axis=0, concat_axis=1, tiled=True)
    return home_rows.reshape(row_count, home_rows.shape[2])


def invert_all(spectra):
    half_width = spectra.shape[3] // 2
    joined = jnp.stack(
        [
            spectra[0, :, :, :half_width] - spectra[1, :, :, half_width:],
            spectra[1, :, :, :half_width] + spectra[0, :, :, half_width:],
        ]
    )
    return inverse_rows(joined)


def shards(signal, grad_out, filter_taps, skip_gain):
    channels = filter_taps.shape[1]
    signal_rows = signal[0].astype(jnp.float32)
    grad_rows = grad_out[0].astype(jnp.float32)
    tap_half = filter_taps.shape[1] // 2
    columns = jnp.concatenate(
        [signal_rows, filter_taps[:, :tap_half], grad_rows, filter_taps[:, tap_half:]], axis=1
    )
    first, second = split_pairs(forward_spectra(columns))
    signal_spec = first[:, :, :, :channels]
    grad_spec = second[:, :, :, :channels]
    own_spec = jnp.concatenate([first[:, :, :, channels:], second[:, :, :, channels:]], axis=3)
    input_spec = jnp.stack(
        [
            grad_spec[0] * own_spec[0] + grad_spec[1] * own_spec[1],
            grad_spec[1] * own_spec[0] - grad_spec[0] * own_spec[1],
        ]
    )
    filter_terms = jnp.stack(
        [
            grad_spec[0] * signal_spec[0] + grad_spec[1] * signal_spec[1],
            grad_spec[1] * signal_spec[0] - grad_spec[0] * signal_spec[1],
        ]
    )
    shared_terms = summed_on_arrival(filter_terms, "batch", 3)
    rows_back = invert_all(jnp.concatenate([input_spec, shared_terms], axis=3))
    filter_grad = gather_directly(rows_back[:, channels:], "batch", 1)
    input_grad = (rows_back[:, :channels] + skip_gain[None, :] * grad_rows).astype(jnp.bfloat16)
    return (input_grad[None], filter_grad)


def solution(mesh):
    return jax.shard_map(
        shards,
        mesh=mesh,
        in_specs=(P("batch", "seq", None), P("batch", "seq", None), P("seq", None), P()),
        out_specs=(P("batch", "seq", None), P("seq", None)),
        check_vma=False,
    )
```

profile of v0, /device:TPU:1, one launch (start us, length us, event | category | flops | bytes accessed | tf_op | source)
XLA Modules:
  0.0 239.2 jit_solution(16720733413574259168)
XLA Ops:
  2.7 1.7 copy.29
  4.4 15.1 %all-to-all-start = ((f32[1,256,768]{2,0,1:T(1,128)}), f32[1,256,768]{2,0,1:T(1,128)S(1)}, u32[]{:S(2)}, u32[]{:S(2)}) async-start(f32[1,256,768]{2,0,1:T(1,128)} %copy.29), calls=%async_computation | async-start | bytes 1572864 | tf_op jit(solution)/shard_map/all_to_all | solution.py:65
  19.7 21.7 %all-to-all-done = f32[1,256,768]{2,0,1:T(1,128)S(1)} async-done(((f32[1,256,768]{2,0,1:T(1,128)}), f32[1,256,768]{2,0,1:T(1,128)S(1)}, u32[]{:S(2)}, u32[]{:S(2)}) %all-to-all-start) | async-done | bytes 786464 | tf_op jit(solution)/shard_map/all_to_all | solution.py:65
  41.4 1.9 reduce
  47.8 2.2 copy.32
  50.0 8.2 %all-to-all-start.1 = ((f32[2,128,4,384]{3,2,0,1:T(4,128)}), f32[2,128,4,384]{3,2,0,1:T(4,128)S(1)}, u32[]{:S(2)}, u32[]{:S(2)}) async-start(f32[2,128,4,384]{3,2,0,1:T(4,128)} %copy.32), calls=%async_computation.1 | async-start | bytes 3145728 | tf_op jit(solution)/shard_map/all_to_all | solution.py:99
  58.2 37.3 %all-to-all-done.1 = f32[2,128,4,384]{3,2,0,1:T(4,128)S(1)} async-done(((f32[2,128,4,384]{3,2,0,1:T(4,128)}), f32[2,128,4,384]{3,2,0,1:T(4,128)S(1)}, u32[]{:S(2)}, u32[]{:S(2)}) %all-to-all-start.1) | async-done | bytes 1572896 | tf_op jit(solution)/shard_map/all_to_all | solution.py:99
  97.4 1.8 fusion.35
  99.6 1.8 fusion.37
  101.4 1.8 convolution_add_fusion
  103.2 1.8 convolution_subtract_fusion
  106.3 7.2 %slice.129 = f32[2,1,256,384]{2,3,0,1:T(8,128)} reverse(f32[2,1,256,384]{2,3,0,1:T(8,128)} %get-tuple-element.22), dimensions={2} | reverse | bytes 1572864 | tf_op jit(solution)/shard_map/slice | solution.py:111
  114.7 7.2 %slice.133 = f32[2,1,256,384]{2,3,1,0:T(8,128)} reverse(f32[2,1,256,384]{2,3,1,0:T(8,128)} %get-tuple-element.23), dimensions={2} | reverse | bytes 1572864 | tf_op jit(solution)/shard_map/slice | solution.py:112
  121.9 8.7 %rev.4 = f32[2,2,256,384]{2,3,1,0:T(8,128)} reverse(f32[2,2,256,384]{2,3,1,0:T(8,128)S(1)} %pad_maximum_fusion), dimensions={1,2} | reverse | bytes 3145728 | tf_op jit(solution)/shard_map/rev | solution.py:113
  130.6 1.5 maximum_bitcast_fusion.1
  135.4 8.5 %all-to-all-start.2 = ((f32[4,2,2,256,64]{3,4,2,1,0:T(8,128)}), f32[4,2,2,256,64]{3,4,2,1,0:T(8,128)S(1)}, u32[]{:S(2)}, u32[]{:S(2)}) async-start(f32[4,2,2,256,64]{3,4,2,1,0:T(8,128)} %copy_bitcast_fusion.1), calls=%async_computation.2 | async-start | bytes 2097152 | tf_op jit(solution)/shard_map/all_to_all | solution.py:15
  144.2 13.2 %all-to-all-done.2 = f32[4,2,2,256,64]{3,4,2,1,0:T(8,128)S(1)} async-done(((f32[4,2,2,256,64]{3,4,2,1,0:T(8,128)}), f32[4,2,2,256,64]{3,4,2,1,0:T(8,128)S(1)}, u32[]{:S(2)}, u32[]{:S(2)}) %all-to-all-start.2) | async-done | bytes 1048608 | tf_op jit(solution)/shard_map/all_to_all | solution.py:15
  157.6 1.4 fusion.31
  160.4 1.4 convolution_add_fusion.2
  161.9 1.5 subtract_bitcast_fusion.1
  164.0 32.6 %all_to_all.61 = f32[2,2,256,160]{3,1,0,2:T(2,128)S(1)} all-to-all(f32[2,2,256,160]{3,1,0,2:T(2,128)S(1)} %copy.41), channel_id=1, replica_groups=mesh['batch'=4,'seq'=64] {'seq'}, dimensions={2} | all-to-all | bytes 1310720 | tf_op jit(solution)/shard_map/all_to_all | solution.py:147
  202.0 22.7 %all_to_all.62 = f32[64,4,320]{2,1,0:T(4,128)S(1)} all-to-all(f32[64,4,320]{2,1,0:T(4,128)S(1)} %copy.49), channel_id=1, replica_groups=mesh['batch'=4,'seq'=64] {'seq'}, dimensions={0} | all-to-all | bytes 655360 | tf_op jit(solution)/shard_map/all_to_all | solution.py:156
  225.6 7.7 %all-to-all-start.5 = ((f32[4,256,64]{1,2,0:T(8,128)}), f32[4,256,64]{1,2,0:T(8,128)S(1)}, u32[]{:S(2)}, u32[]{:S(2)}) async-start(f32[4,256,64]{1,2,0:T(8,128)} %broadcast_in_dim.5), calls=%async_computation.5 | async-start | bytes 524288 | tf_op jit(solution)/shard_map/all_to_all | solution.py:21
  234.0 4.3 %all-to-all-done.5 = f32[4,256,64]{1,2,0:T(8,128)S(1)} async-done(((f32[4,256,64]{1,2,0:T(8,128)}), f32[4,256,64]{1,2,0:T(8,128)S(1)}, u32[]{:S(2)}, u32[]{:S(2)}) %all-to-all-start.5) | async-done | bytes 262176 | tf_op jit(solution)/shard_map/all_to_all | solution.py:21
  (69 shorter events, 24.9 us)
Async XLA Ops:
  4.4 37.0 %all-to-all-start = ((f32[1,256,768]{2,0,1:T(1,128)}), f32[1,256,768]{2,0,1:T(1,128)S(1)}, u32[]{:S(2)}, u32[]{:S(2)}) async-start(f32[1,256,768]{2,0,1:T(1,128)} %copy.29), calls=%async_computation | async-start | bytes 1572864 | tf_op jit(solution)/shard_map/all_to_all | solution.py:65
  19.6 26.9 %copy-start.2 = (s32[128]{0:T(128)}, s32[128]{0:T(128)S(1)}, u32[]{:S(2)}) copy-start(s32[128]{0:T(128)S(1)} %get-tuple-element.44) | copy-start | bytes 1540
  19.6 26.9 %copy-start.4 = (s32[128]{0:T(128)}, s32[128]{0:T(128)S(1)}, u32[]{:S(2)}) copy-start(s32[128]{0:T(128)S(1)} %get-tuple-element.45) | copy-start | bytes 1540
  50.0 45.6 %all-to-all-start.1 = ((f32[2,128,4,384]{3,2,0,1:T(4,128)}), f32[2,128,4,384]{3,2,0,1:T(4,128)S(1)}, u32[]{:S(2)}, u32[]{:S(2)}) async-start(f32[2,128,4,384]{3,2,0,1:T(4,128)} %copy.32), calls=%async_computation.1 | async-start | bytes 3145728 | tf_op jit(solution)/shard_map/all_to_all | solution.py:99
  130.6 1.6 copy-start
  135.4 22.0 %all-to-all-start.2 = ((f32[4,2,2,256,64]{3,4,2,1,0:T(8,128)}), f32[4,2,2,256,64]{3,4,2,1,0:T(8,128)S(1)}, u32[]{:S(2)}, u32[]{:S(2)}) async-start(f32[4,2,2,256,64]{3,4,2,1,0:T(8,128)} %copy_bitcast_fusion.1), calls=%async_computation.2 | async-start | bytes 2097152 | tf_op jit(solution)/shard_map/all_to_all | solution.py:15
  197.0 0.8 copy-start.3
  197.0 0.8 copy-start.5
  202.0 31.3 %copy-start.1 = (bf16[1,256,256]{2,1,0:T(8,128)(2,1)S(1)}, bf16[1,256,256]{2,1,0:T(8,128)(2,1)}, u32[]{:S(2)}) copy-start(bf16[1,256,256]{2,1,0:T(8,128)(2,1)} %param.5) | copy-start | bytes 393220
  202.0 31.3 %copy-start.6 = (f32[256]{0:T(256)S(1)}, f32[256]{0:T(256)}, u32[]{:S(2)}) copy-start(f32[256]{0:T(256)} %param.7) | copy-start | bytes 3076
  225.6 12.7 %all-to-all-start.5 = ((f32[4,256,64]{1,2,0:T(8,128)}), f32[4,256,64]{1,2,0:T(8,128)S(1)}, u32[]{:S(2)}, u32[]{:S(2)}) async-start(f32[4,256,64]{1,2,0:T(8,128)} %broadcast_in_dim.5), calls=%async_computation.5 | async-start | bytes 524288 | tf_op jit(solution)/shard_map/all_to_all | solution.py:21
where the time goes:
time: 241 us; the launch traced here: 239 us
  waiting for transfers between devices  76.6 us (32%)
  blocking collectives  55.3 us (23%)
  starting transfers between devices  39.6 us (16%)
  local copies, waits for them, and re-layouts  36.1 us (15%)
  matrix products  20.2 us (8%)
  other arithmetic  10.4 us (4%)
    all_to_all x1, waiting for transfers between devices, forward_spectra(): lax.all_to_all(rotated, 'seq', split_axis=1, concat_axis=2, tiled=True)  37.3 us
    all_to_all x1, blocking collectives, inverse_rows(): lax.all_to_all(rotated, 'seq', split_axis=2, concat_axis=1, tiled=True)  32.6 us
    all_to_all x1, blocking collectives, inverse_rows(): lax.all_to_all(gathered, 'seq', split_axis=0, concat_axis=1, tiled=True)  22.7 us
    all_to_all x1, waiting for transfers between devices, forward_spectra(): lax.all_to_all(columns.reshape(1, row_count, columns.shape[1]), 'seq', sp...  21.7 us
    dot_general x16, matrix products, contract(): return jnp.einsum(form, table, operand, precision=lax.Precision.HIGHEST)  20.2 us
    all_to_all x1, starting transfers between devices, forward_spectra(): lax.all_to_all(columns.reshape(1, row_count, columns.shape[1]), 'seq', sp...  15.1 us
    all_to_all x1, waiting for transfers between devices, summed_on_arrival(): lax.all_to_all(parts, axis, split_axis=0, concat_axis=0, tiled=True)  13.2 us
    rev x1, local copies, waits for them, and re-layouts, split_pairs(): reversed_q[:, ::-1]  8.74 us
  transfers between devices with their start and end apart: 4, of which 4 were waited for; matrix products, arithmetic and copies ran while one was open for 0% of the time, Pallas kernels for 0%

commit v1 on v0

v1 whole, which is shorter than its diff:
```python
import ml_dtypes
import numpy as np
import jax
import jax.numpy as jnp
from jax import lax
from jax.experimental import pallas as pl
from jax.experimental.pallas import tpu as pltpu
from jax.sharding import PartitionSpec as P


F32 = jnp.float32
BF16 = jnp.bfloat16
SIDE = 128
LEN = SIDE * SIDE
MESH = pl.DeviceIdType.MESH
TAPS, GRAD, SIGNAL, INPUT, FILTER, SWAP_GRAD, SWAP_SIGNAL, SWAP_INPUT, SWAP_FILTER = range(9)


def split_table(table):
    high = table.astype(np.float32).astype(ml_dtypes.bfloat16)
    low = (table - high.astype(np.float64)).astype(np.float32).astype(ml_dtypes.bfloat16)
    return high, low


def tables():
    index = np.arange(SIDE)
    angle = 2 * np.pi * (np.outer(4 * index + 1, index) % (4 * SIDE)) / (4.0 * SIDE)
    high, low = split_table(np.concatenate([np.cos(angle), -np.sin(angle)], axis=0))
    first = np.concatenate([high, low, high], axis=1)
    fine = 2 * np.pi * (np.outer(index, index) % SIDE) / float(SIDE)
    cos_fine, sin_fine = np.cos(fine), np.sin(fine)
    second = np.stack(split_table(np.block([[cos_fine, -sin_fine], [sin_fine, cos_fine]])))
    third = np.stack(split_table(np.block([[cos_fine, sin_fine], [-sin_fine, cos_fine]])))
    fourth = np.stack(split_table(np.concatenate([np.cos(angle.T), -np.sin(angle.T)], axis=1) / LEN))
    turn = 2 * np.pi * np.outer(4 * index + 1, index) / (4.0 * LEN)
    turns = np.stack([np.cos(turn), np.sin(turn)]).astype(np.float32)
    return tuple(jnp.asarray(table) for table in (first, second, third, fourth, turns))


def split(value):
    high = value.astype(BF16)
    return high, (value - high.astype(F32)).astype(BF16)


def dot(left, right):
    return jnp.dot(left, right, preferred_element_type=F32)


def body(
    signal, grad, taps, gain, first, second, third, fourth, turns,
    out_input, out_filter,
    send_taps, send_grad, send_signal, stage_grad, stage_signal, land_taps, land_grad, land_signal,
    send_input, send_filter, land_input, land_filter, pair_input, pair_filter,
    coarse, rows_high, rows_low, spectra, columns_high, columns_low,
    sends, recvs,
):
    batch = lax.axis_index("batch")
    seq = lax.axis_index("seq")
    core = batch % 2
    x_low = batch // 2
    x_pos = 2 * ((seq // 8) % 2) + x_low
    y_pos = seq // 16
    z_pos = seq % 8
    me = x_low * 64 + seq
    partner = (batch + 1 - 2 * core, seq)
    own = pl.multiple_of(core * SIDE, SIDE)
    other = pl.multiple_of((1 - core) * SIDE, SIDE)

    def each_peer(act):
        for dz in (4, 3, 5, 2, 6, 1, 7, 0):

            def one(step, carry, dz=dz):
                x_to = (x_pos + step % 4) % 4
                y_to = (y_pos + step // 4) % 4
                z_to = (z_pos + dz * (1 - 2 * core) + 8) % 8
                act(x_to % 2, y_to * 16 + (x_to // 2) * 8 + z_to)
                return carry

            lax.fori_loop(1 if dz == 0 else 0, 16, one, 0)

    def copy(source, landing, slot, device):
        return pltpu.make_async_remote_copy(
            src_ref=source, dst_ref=landing, send_sem=sends.at[slot], recv_sem=recvs.at[slot],
            device_id=device, device_id_type=MESH,
        )

    def send_all(source_of, landing, slot):
        each_peer(
            lambda x, s: copy(source_of(x, s), landing, slot, (2 * x + core, s)).start()
        )

    barrier = pltpu.get_barrier_semaphore()
    each_peer(
        lambda x, s: pl.semaphore_signal(
            barrier, inc=1, device_id=(2 * x + core, s), device_id_type=MESH
        )
    )
    pl.semaphore_signal(barrier, inc=1, device_id=partner, device_id_type=MESH)

    for array, stage, send in ((grad, stage_grad, send_grad), (signal, stage_signal, send_signal)):
        for half in range(2):
            rows = pl.ds(half * SIDE, SIDE)
            spread = pl.ds(half, SIDE, stride=2)
            stage[spread, :] = array[rows, pl.ds(other, SIDE)].astype(F32).T
            send[core, spread, :] = array[rows, pl.ds(own, SIDE)].astype(F32).T
    send_taps[...] = taps[pl.ds(pl.multiple_of(x_low * SIDE, SIDE), SIDE), pl.ds(own, SIDE)].T
    pl.semaphore_wait(barrier, 128)

    swap_grad = copy(stage_grad, send_grad.at[core], SWAP_GRAD, partner)
    swap_signal = copy(stage_signal, send_signal.at[core], SWAP_SIGNAL, partner)
    swap_grad.start()
    swap_signal.start()

    taps_at = land_taps.at[pl.ds(2 * seq + x_low, 1)]
    send_all(lambda x, s: send_taps.at[pl.ds(64 * x + s, 1)], taps_at, TAPS)
    land_taps[pl.ds(2 * seq + x_low, 1), :] = send_taps[pl.ds(me, 1), :]

    for swap, send, land, slot in (
        (swap_grad, send_grad, land_grad, GRAD),
        (swap_signal, send_signal, land_signal, SIGNAL),
    ):
        swap.wait()
        send_all(
            lambda x, s, send=send: send.at[:, pl.ds(2 * (64 * x + s), 2), :],
            land.at[pl.ds(2 * x_low, 2), pl.ds(2 * seq, 2), :],
            slot,
        )
        for b in range(2):
            land[2 * x_low + b, pl.ds(2 * seq, 2), :] = send[b, pl.ds(2 * me, 2), :]

    all_taps = copy(land_taps.at[pl.ds(0, 127)], land_taps.at[pl.ds(0, 127)], TAPS, partner)
    all_grad, all_signal = (
        copy(land.at[:, pl.ds(0, 127), :], land.at[:, pl.ds(0, 127), :], slot, partner)
        for land, slot in ((land_grad, GRAD), (land_signal, SIGNAL))
    )

    cos_turn, sin_turn = turns[0], turns[1]

    def turn_forward(count):
        for b in range(count):
            real = coarse[:SIDE, b * SIDE : (b + 1) * SIDE]
            imag = coarse[SIDE:, b * SIDE : (b + 1) * SIDE]
            rows = pl.ds(b * SIDE, SIDE)
            rows_high[rows, :SIDE], rows_low[rows, :SIDE] = split(real * cos_turn + imag * sin_turn)
            rows_high[rows, SIDE:], rows_low[rows, SIDE:] = split(imag * cos_turn - real * sin_turn)

    def along_rows(table, count):
        rows = pl.ds(0, count * SIDE)
        return (
            dot(rows_high[rows, :], table[0])
            + dot(rows_low[rows, :], table[0])
            + dot(rows_high[rows, :], table[1])
        )

    def exact_columns(land):
        columns = jnp.concatenate([land[b].astype(BF16) for b in range(4)], axis=1)
        return dot(first[:, : 2 * SIDE], jnp.concatenate([columns, columns], axis=0))

    def inverse(products, count):
        for b in range(count):
            real, imag = products[b]
            rows = pl.ds(b * SIDE, SIDE)
            rows_high[rows, :SIDE], rows_low[rows, :SIDE] = split(real)
            rows_high[rows, SIDE:], rows_low[rows, SIDE:] = split(imag)
        lines = along_rows(third, count)
        for b in range(count):
            real = lines[b * SIDE : (b + 1) * SIDE, :SIDE]
            imag = lines[b * SIDE : (b + 1) * SIDE, SIDE:]
            where = pl.ds(b * SIDE, SIDE)
            columns_high[:SIDE, where], columns_low[:SIDE, where] = split(real * cos_turn - imag * sin_turn)
            columns_high[SIDE:, where], columns_low[SIDE:, where] = split(real * sin_turn + imag * cos_turn)
        where = pl.ds(0, count * SIDE)
        return (
            dot(fourth[0], columns_high[:, where])
            + dot(fourth[0], columns_low[:, where])
            + dot(fourth[1], columns_high[:, where])
        )

    def times_conjugate(left, right):
        return (
            left[0] * right[0] + left[1] * right[1],
            left[1] * right[0] - left[0] * right[1],
        )

    def spectrum(b):
        rows = pl.ds(b * SIDE, SIDE)
        return spectra[rows, :SIDE], spectra[rows, SIDE:]

    all_taps.wait()
    taps_high, taps_low = split(land_taps[...])
    coarse[:, 4 * SIDE :] = dot(first[...], jnp.concatenate([taps_high, taps_high, taps_low], axis=0))
    all_grad.wait()
    coarse[:, : 4 * SIDE] = exact_columns(land_grad)
    turn_forward(5)
    spectra[...] = along_rows(second, 5)
    filter_spectrum = spectrum(4)
    values = inverse([times_conjugate(spectrum(b), filter_spectrum) for b in range(4)], 4)
    for b in range(4):
        send_input[b] = values[:, b * SIDE : (b + 1) * SIDE]
    send_all(
        lambda x, s: send_input.at[pl.ds(2 * x, 2), pl.ds(2 * s, 2), :],
        land_input.at[:, pl.ds(2 * me, 2), :],
        INPUT,
    )
    for b in range(2):
        land_input[b, pl.ds(2 * me, 2), :] = send_input[2 * x_low + b, pl.ds(2 * seq, 2), :]

    all_signal.wait()
    coarse[:, : 4 * SIDE] = exact_columns(land_signal)
    turn_forward(4)
    signal_spectra = along_rows(second, 4)
    total_real, total_imag = 0.0, 0.0
    for b in range(4):
        lines = signal_spectra[b * SIDE : (b + 1) * SIDE]
        real, imag = times_conjugate(spectrum(b), (lines[:, :SIDE], lines[:, SIDE:]))
        total_real, total_imag = total_real + real, total_imag + imag
    send_filter[...] = inverse([(total_real, total_imag)], 1)
    send_all(
        lambda x, s: send_filter.at[pl.ds(2 * s, 2), :], land_filter.at[pl.ds(2 * me, 2), :], FILTER
    )
    land_filter[pl.ds(2 * me, 2), :] = send_filter[pl.ds(2 * seq, 2), :]

    all_input = copy(land_input.at[:, pl.ds(0, 254), :], land_input.at[:, pl.ds(0, 254), :], INPUT, partner)
    all_input.wait()
    swap_input = copy(land_input.at[1 - core], pair_input, SWAP_INPUT, partner)
    swap_input.start()

    def finish_input(block_of, lanes):
        for half in range(2):
            rows = pl.ds(half * SIDE, SIDE)
            skip = gain[:, pl.ds(lanes, SIDE)] * grad[rows, pl.ds(lanes, SIDE)].astype(F32)
            out_input[rows, pl.ds(lanes, SIDE)] = (block_of(half).T + skip).astype(BF16)

    finish_input(lambda half: land_input[core, pl.ds(half, SIDE, stride=2), :], own)
    swap_input.wait()
    finish_input(lambda half: pair_input[pl.ds(half, SIDE, stride=2), :], other)

    all_filter = copy(land_filter.at[pl.ds(0, 254)], land_filter.at[pl.ds(0, 254)], FILTER, partner)
    all_filter.wait()
    swap_filter = copy(land_filter, pair_filter, SWAP_FILTER, partner)
    swap_filter.start()
    for half in range(2):
        out_filter[pl.ds(half * SIDE, SIDE), pl.ds(own, SIDE)] = land_filter[pl.ds(half, SIDE, stride=2), :].T
    swap_filter.wait()
    for half in range(2):
        out_filter[pl.ds(half * SIDE, SIDE), pl.ds(other, SIDE)] = pair_filter[pl.ds(half, SIDE, stride=2), :].T


def shards(signal, grad_out, filter_taps, skip_gain):
    vmem = pl.BlockSpec(memory_space=pltpu.VMEM)
    rows = lambda *shape: pltpu.VMEM((*shape, SIDE), F32)
    input_grad, filter_grad = pl.pallas_call(
        body,
        out_shape=(
            jax.ShapeDtypeStruct((2 * SIDE, 2 * SIDE), BF16),
            jax.ShapeDtypeStruct((2 * SIDE, 2 * SIDE), F32),
        ),
        in_specs=[vmem] * 9,
        out_specs=(vmem, vmem),
        scratch_shapes=[
            rows(SIDE), rows(2, 2 * SIDE), rows(2, 2 * SIDE), rows(2 * SIDE), rows(2 * SIDE),
            rows(SIDE), rows(4, SIDE), rows(4, SIDE),
            rows(4, SIDE), rows(SIDE), rows(2, 2 * SIDE), rows(2 * SIDE), rows(2 * SIDE), rows(2 * SIDE),
            pltpu.VMEM((2 * SIDE, 5 * SIDE), F32),
            pltpu.VMEM((5 * SIDE, 2 * SIDE), BF16),
            pltpu.VMEM((5 * SIDE, 2 * SIDE), BF16),
            pltpu.VMEM((5 * SIDE, 2 * SIDE), F32),
            pltpu.VMEM((2 * SIDE, 4 * SIDE), BF16),
            pltpu.VMEM((2 * SIDE, 4 * SIDE), BF16),
            pltpu.SemaphoreType.DMA((9,)),
            pltpu.SemaphoreType.DMA((9,)),
        ],
        compiler_params=pltpu.CompilerParams(collective_id=0, has_side_effects=True),
    )(signal[0], grad_out[0], filter_taps, skip_gain[None, :], *tables())
    return input_grad[None], filter_grad


def solution(mesh):
    return jax.shard_map(
        shards,
        mesh=mesh,
        in_specs=(P("batch", "seq", None), P("batch", "seq", None), P("seq", None), P()),
        out_specs=(P("batch", "seq", None), P("seq", None)),
        check_vma=False,
    )
```

time: 241 us -> 50.7 us (0.21)
  waiting for transfers between devices: 76.6 us -> 0 us
  blocking collectives: 55.3 us -> 0 us
  Pallas kernels: 0 us -> 47.6 us
  starting transfers between devices: 39.6 us -> 0 us
  local copies, waits for them, and re-layouts: 36.1 us -> 2.32 us
  matrix products: 20.2 us -> 0 us
  other arithmetic: 10.4 us -> 0 us
    all_to_all x4 -> x0, waiting for transfers between devices: 76.6 us -> none  [the longest x1 37.3 us: forward_spectra(): lax.all_to_all(rotated, 'seq', split_axis=1, concat_axis=2, tiled=True)]
    all_to_all x2 -> x0, blocking collectives: 55.3 us -> none  [the longest x1 32.6 us: inverse_rows(): lax.all_to_all(rotated, 'seq', split_axis=2, concat_axis=1, tiled=True)]
    pallas_call x0 -> x1, Pallas kernels: none -> 47.6 us  [shards(): pl.pallas_call(body, out_shape=(jax.ShapeDtypeStruct((2 * SIDE, 2 * SIDE)...]
    all_to_all x4 -> x0, starting transfers between devices: 39.6 us -> none  [the longest x1 15.1 us: forward_spectra(): lax.all_to_all(columns.reshape(1, row_count, columns.shape[1]), 'seq', sp...]
    dot_general x16 -> x0, matrix products: 20.2 us -> none  [contract(): return jnp.einsum(form, table, operand, precision=lax.Precision.HIGHEST)]
    slice x11 -> x0, local copies, waits for them, and re-layouts: 17.9 us -> none  [the longest x2 8.35 us: split_pairs(): zero_row = jnp.roll(reversed_q[:, 0], 1, axis=1)]
    rev x1 -> x0, local copies, waits for them, and re-layouts: 8.74 us -> none  [split_pairs(): reversed_q[:, ::-1]]
    another operation x2 -> x0, local copies, waits for them, and re-layouts: 2.79 us -> none  [the longest x1 2.19 us: forward_spectra(): jnp.stack([real_part * cos_turn + imag_part * sin_turn, imag_part * cos_t...]
  transfers between devices with their start and end apart: 4 -> 0, of which waited for: 4 -> 0; matrix products, arithmetic and copies ran while one was open for 0% -> 0% of each run, Pallas kernels for 0% -> 0%
where the time goes in v1:
time: 50.7 us; the launch traced here: 50.6 us
  Pallas kernels  47.6 us (94%)
  local copies, waits for them, and re-layouts  2.32 us (5%)
  between operations  0.65 us (1%)
    pallas_call x1, Pallas kernels, shards(): pl.pallas_call(body, out_shape=(jax.ShapeDtypeStruct((2 * SIDE, 2 * SIDE)...  47.6 us
    unnamed x4, local copies, waits for them, and re-layouts  2.32 us

profile of v1, /device:TPU:1, one launch (start us, length us, event | category | flops | bytes accessed | tf_op | source)
XLA Modules:
  0.0 50.6 jit_solution(5580978840824709850)
XLA Ops:
  0.6 47.6 %shard_map.104 = (bf16[256,256]{1,0:T(8,128)(2,1)}, f32[256,256]{1,0:T(8,128)}) custom-call(bf16[256,256]{1,0:T(8,128)(2,1)} %bitcast.4, bf16[256,256]{1,0:T(8,128)(2,1)} %bitcast.5, f32[256,256]{1,0:T(8,128)} %taps.1, f32[1,256]{1,0:T(1,128)} %bitcast.7, bf16[256,384]{1,0:T(8,128)(2,1)} %constant.10.clone.first, ...), custom_call_target="tpu_custom_call" | custom-call | tf_op jit(solution)/shard_map/pallas_call | solution.py:252
  48.3 0.0 copy-start
  48.3 1.6 %copy.13 = bf16[1,256,256]{2,1,0:T(8,128)(2,1)} copy(bf16[1,256,256]{2,1,0:T(8,128)(2,1)} %bitcast.6) | data formatting | bytes 262144
  49.9 0.0 copy-done
  49.9 0.7 %copy.14 = f32[256,256]{1,0:T(8,128)} copy(f32[256,256]{1,0:T(8,128)S(1)} %copy-done) | data formatting | bytes 524288
Async XLA Ops:
  48.3 1.6 %copy-start = (f32[256,256]{1,0:T(8,128)S(1)}, f32[256,256]{1,0:T(8,128)}, u32[]{:S(2)}) copy-start(f32[256,256]{1,0:T(8,128)} %get-tuple-element.9) | copy-start | bytes 786436

commit v2 on v1

--- a/solution.py
+++ b/solution.py
@@ -47,12 +47,23 @@
 
 
 def body(
-    signal, grad, taps, gain, first, second, third, fourth, turns,
+    signal_far, grad_far, taps_far, gain_far, *rest
+):
+    (
+        tables_far, (out_input, out_filter), (signal, grad, taps, gain), held_tables, rest
+    ) = rest[:5], rest[5:7], rest[7:11], rest[11:16], rest[16:]
+    run(signal_far, grad_far, taps_far, gain_far, tables_far, out_input, out_filter,
+        signal, grad, taps, gain, *held_tables, held_tables, *rest)
+
+
+def run(
+    signal_far, grad_far, taps_far, gain_far, tables_far,
     out_input, out_filter,
+    signal, grad, taps, gain, first, second, third, fourth, turns, held_tables,
     send_taps, send_grad, send_signal, stage_grad, stage_signal, land_taps, land_grad, land_signal,
     send_input, send_filter, land_input, land_filter, pair_input, pair_filter,
     coarse, rows_high, rows_low, spectra, columns_high, columns_low,
-    sends, recvs,
+    sends, recvs, loads,
 ):
     batch = lax.axis_index("batch")
     seq = lax.axis_index("seq")
@@ -89,6 +100,19 @@
             lambda x, s: copy(source_of(x, s), landing, slot, (2 * x + core, s)).start()
         )
 
+    x_rows = pl.ds(pl.multiple_of(x_low * SIDE, SIDE), SIDE)
+    load_grad, load_signal, load_taps, load_gain, *load_tables = [
+        pltpu.make_async_copy(far, near, loads.at[slot])
+        for slot, (far, near) in enumerate(
+            [
+                (grad_far, grad), (signal_far, signal), (taps_far.at[x_rows, pl.ds(own, SIDE)], taps),
+                (gain_far, gain), *zip(tables_far, held_tables),
+            ]
+        )
+    ]
+    for load in (load_grad, load_signal, load_taps, load_gain, *load_tables):
+        load.start()
+
     barrier = pltpu.get_barrier_semaphore()
     each_peer(
         lambda x, s: pl.semaphore_signal(
@@ -97,13 +121,17 @@
     )
     pl.semaphore_signal(barrier, inc=1, device_id=partner, device_id_type=MESH)
 
-    for array, stage, send in ((grad, stage_grad, send_grad), (signal, stage_signal, send_signal)):
+    for load, array, stage, send in (
+        (load_grad, grad, stage_grad, send_grad), (load_signal, signal, stage_signal, send_signal)
+    ):
+        load.wait()
         for half in range(2):
             rows = pl.ds(half * SIDE, SIDE)
             spread = pl.ds(half, SIDE, stride=2)
             stage[spread, :] = array[rows, pl.ds(other, SIDE)].astype(F32).T
             send[core, spread, :] = array[rows, pl.ds(own, SIDE)].astype(F32).T
-    send_taps[...] = taps[pl.ds(pl.multiple_of(x_low * SIDE, SIDE), SIDE), pl.ds(own, SIDE)].T
+    load_taps.wait()
+    send_taps[...] = taps[...].T
     pl.semaphore_wait(barrier, 128)
 
     swap_grad = copy(stage_grad, send_grad.at[core], SWAP_GRAD, partner)
@@ -134,6 +162,8 @@
         for land, slot in ((land_grad, GRAD), (land_signal, SIGNAL))
     )
 
+    for load in (load_gain, *load_tables):
+        load.wait()
     cos_turn, sin_turn = turns[0], turns[1]
 
     def turn_forward(count):
@@ -248,16 +278,22 @@
 
 def shards(signal, grad_out, filter_taps, skip_gain):
     vmem = pl.BlockSpec(memory_space=pltpu.VMEM)
+    held = tables()
     rows = lambda *shape: pltpu.VMEM((*shape, SIDE), F32)
     input_grad, filter_grad = pl.pallas_call(
         body,
         out_shape=(
-            jax.ShapeDtypeStruct((2 * SIDE, 2 * SIDE), BF16),
-            jax.ShapeDtypeStruct((2 * SIDE, 2 * SIDE), F32),
+            pltpu.VMEM((2 * SIDE, 2 * SIDE), BF16),
+            pltpu.VMEM((2 * SIDE, 2 * SIDE), F32),
         ),
-        in_specs=[vmem] * 9,
+        in_specs=[pl.BlockSpec(memory_space=pl.ANY)] * 9,
         out_specs=(vmem, vmem),
         scratch_shapes=[
+            pltpu.VMEM((2 * SIDE, 2 * SIDE), BF16),
+            pltpu.VMEM((2 * SIDE, 2 * SIDE), BF16),
+            rows(SIDE),
+            pltpu.VMEM((1, 2 * SIDE), F32),
+            *(pltpu.VMEM(table.shape, table.dtype) for table in held),
             rows(SIDE), rows(2, 2 * SIDE), rows(2, 2 * SIDE), rows(2 * SIDE), rows(2 * SIDE),
             rows(SIDE), rows(4, SIDE), rows(4, SIDE),
             rows(4, SIDE), rows(SIDE), rows(2, 2 * SIDE), rows(2 * SIDE), rows(2 * SIDE), rows(2 * SIDE),
@@ -269,9 +305,10 @@
             pltpu.VMEM((2 * SIDE, 4 * SIDE), BF16),
             pltpu.SemaphoreType.DMA((9,)),
             pltpu.SemaphoreType.DMA((9,)),
+            pltpu.SemaphoreType.DMA((9,)),
         ],
         compiler_params=pltpu.CompilerParams(collective_id=0, has_side_effects=True),
-    )(signal[0], grad_out[0], filter_taps, skip_gain[None, :], *tables())
+    )(signal[0], grad_out[0], filter_taps, skip_gain[None, :], *held)
     return input_grad[None], filter_grad
 
 

time: 50.7 us -> 48.5 us (0.957)
  Pallas kernels: 47.6 us -> 46.4 us
  local copies, waits for them, and re-layouts: 2.32 us -> 1.36 us
    pallas_call x1, Pallas kernels: 47.6 us -> 46.4 us  [shards(): pl.pallas_call(body, out_shape=(pltpu.VMEM((2 * SIDE, 2 * SIDE), BF16), p...]
    unnamed x4 -> x2, local copies, waits for them, and re-layouts: 2.32 us -> 1.36 us
where the time goes in v2:
time: 48.5 us; the launch traced here: 48.4 us
  Pallas kernels  46.4 us (96%)
  local copies, waits for them, and re-layouts  1.36 us (3%)
  between operations  0.64 us (1%)
    pallas_call x1, Pallas kernels, shards(): pl.pallas_call(body, out_shape=(pltpu.VMEM((2 * SIDE, 2 * SIDE), BF16), p...  46.4 us
    unnamed x2, local copies, waits for them, and re-layouts  1.36 us

profile of v2, /device:TPU:1, one launch (start us, length us, event | category | flops | bytes accessed | tf_op | source)
XLA Modules:
  0.0 48.4 jit_solution(9552870940126050031)
XLA Ops:
  0.6 46.4 %shard_map.104 = (bf16[256,256]{1,0:T(8,128)(2,1)S(1)}, f32[256,256]{1,0:T(8,128)S(1)}) custom-call(bf16[256,256]{1,0:T(8,128)(2,1)} %bitcast.5, bf16[256,256]{1,0:T(8,128)(2,1)} %bitcast.6, f32[256,256]{1,0:T(8,128)} %taps_far.1, f32[1,256]{1,0:T(1,128)} %bitcast.7, bf16[256,384]{1,0:T(8,128)(2,1)} %constant.10.clone.rest_0_, ...), custom_call_target="tpu_custom_call" | custom-call | tf_op jit(solution)/shard_map/pallas_call | solution.py:283
  47.1 0.7 %copy.13 = bf16[1,256,256]{2,1,0:T(8,128)(2,1)} copy(bf16[1,256,256]{2,1,0:T(8,128)(2,1)S(1)} %bitcast.4) | data formatting | bytes 262144
  47.7 0.7 %copy.14 = f32[256,256]{1,0:T(8,128)} copy(f32[256,256]{1,0:T(8,128)S(1)} %get-tuple-element.7) | data formatting | bytes 524288

commit v3 on v2

--- a/solution.py
+++ b/solution.py
@@ -12,7 +12,7 @@
 BF16 = jnp.bfloat16
 SIDE = 128
 LEN = SIDE * SIDE
-MESH = pl.DeviceIdType.MESH
+LOGICAL = pl.DeviceIdType.LOGICAL
 TAPS, GRAD, SIGNAL, INPUT, FILTER, SWAP_GRAD, SWAP_SIGNAL, SWAP_INPUT, SWAP_FILTER = range(9)
 
 
@@ -73,32 +73,39 @@
     y_pos = seq // 16
     z_pos = seq % 8
     me = x_low * 64 + seq
-    partner = (batch + 1 - 2 * core, seq)
+    partner = (batch + 1 - 2 * core) * 64 + seq
     own = pl.multiple_of(core * SIDE, SIDE)
     other = pl.multiple_of((1 - core) * SIDE, SIDE)
 
+    sign = 1 - 2 * core
+    bases = []
+    for step in range(16):
+        x_to = (x_pos + step % 4) % 4
+        place = ((y_pos + step // 4) % 4) * 16 + (x_to // 2) * 8
+        bases.append((x_to % 2, place, place + (x_to % 2) * 128 + core * 64))
+
     def each_peer(act):
-        for dz in (4, 3, 5, 2, 6, 1, 7, 0):
-
-            def one(step, carry, dz=dz):
-                x_to = (x_pos + step % 4) % 4
-                y_to = (y_pos + step // 4) % 4
-                z_to = (z_pos + dz * (1 - 2 * core) + 8) % 8
-                act(x_to % 2, y_to * 16 + (x_to // 2) * 8 + z_to)
-                return carry
-
-            lax.fori_loop(1 if dz == 0 else 0, 16, one, 0)
+        def some(near, far, first):
+            for dz, start in ((near, 0), (far, first)):
+                z_to = (z_pos + sign * dz + 8) % 8
+                for x, place, device in bases[start:]:
+                    act(x, place + z_to, device + z_to)
+
+        def several(step, carry):
+            some(4 - step, 5 + step, 0)
+            return carry
+
+        lax.fori_loop(0, 3, several, 0)
+        some(1, 0, 1)
 
     def copy(source, landing, slot, device):
         return pltpu.make_async_remote_copy(
             src_ref=source, dst_ref=landing, send_sem=sends.at[slot], recv_sem=recvs.at[slot],
-            device_id=device, device_id_type=MESH,
+            device_id=device, device_id_type=LOGICAL,
         )
 
     def send_all(source_of, landing, slot):
-        each_peer(
-            lambda x, s: copy(source_of(x, s), landing, slot, (2 * x + core, s)).start()
-        )
+        each_peer(lambda x, s, device: copy(source_of(x, s), landing, slot, device).start())
 
     x_rows = pl.ds(pl.multiple_of(x_low * SIDE, SIDE), SIDE)
     load_grad, load_signal, load_taps, load_gain, *load_tables = [
@@ -115,11 +122,11 @@
 
     barrier = pltpu.get_barrier_semaphore()
     each_peer(
-        lambda x, s: pl.semaphore_signal(
-            barrier, inc=1, device_id=(2 * x + core, s), device_id_type=MESH
-        )
-    )
-    pl.semaphore_signal(barrier, inc=1, device_id=partner, device_id_type=MESH)
+        lambda x, s, device: pl.semaphore_signal(
+            barrier, inc=1, device_id=device, device_id_type=LOGICAL
+        )
+    )
+    pl.semaphore_signal(barrier, inc=1, device_id=partner, device_id_type=LOGICAL)
 
     for load, array, stage, send in (
         (load_grad, grad, stage_grad, send_grad), (load_signal, signal, stage_signal, send_signal)
@@ -149,7 +156,7 @@
     ):
         swap.wait()
         send_all(
-            lambda x, s, send=send: send.at[:, pl.ds(2 * (64 * x + s), 2), :],
+            lambda x, s, send=send: send.at[:, pl.ds(128 * x + 2 * s, 2), :],
             land.at[pl.ds(2 * x_low, 2), pl.ds(2 * seq, 2), :],
             slot,
         )

time: 48.5 us -> 44.1 us (0.909)
  Pallas kernels: 46.4 us -> 42 us
    pallas_call x1, Pallas kernels: 46.4 us -> 42 us  [shards(): pl.pallas_call(body, out_shape=(pltpu.VMEM((2 * SIDE, 2 * SIDE), BF16), p...]
where the time goes in v3:
time: 44.1 us; the launch traced here: 44 us
  Pallas kernels  42 us (95%)
  local copies, waits for them, and re-layouts  1.36 us (3%)
  between operations  0.64 us (1%)
    pallas_call x1, Pallas kernels, shards(): pl.pallas_call(body, out_shape=(pltpu.VMEM((2 * SIDE, 2 * SIDE), BF16), p...  42 us
    unnamed x2, local copies, waits for them, and re-layouts  1.36 us

profile of v3, /device:TPU:1, one launch (start us, length us, event | category | flops | bytes accessed | tf_op | source)
XLA Modules:
  0.0 44.0 jit_solution(14404163501950566094)
XLA Ops:
  0.6 42.0 %shard_map.104 = (bf16[256,256]{1,0:T(8,128)(2,1)S(1)}, f32[256,256]{1,0:T(8,128)S(1)}) custom-call(bf16[256,256]{1,0:T(8,128)(2,1)} %bitcast.5, bf16[256,256]{1,0:T(8,128)(2,1)} %bitcast.6, f32[256,256]{1,0:T(8,128)} %taps_far.1, f32[1,256]{1,0:T(1,128)} %bitcast.7, bf16[256,384]{1,0:T(8,128)(2,1)} %constant.10.clone.rest_0_, ...), custom_call_target="tpu_custom_call" | custom-call | tf_op jit(solution)/shard_map/pallas_call | solution.py:290
  42.7 0.7 %copy.13 = bf16[1,256,256]{2,1,0:T(8,128)(2,1)} copy(bf16[1,256,256]{2,1,0:T(8,128)(2,1)S(1)} %bitcast.4) | data formatting | bytes 262144
  43.3 0.7 %copy.14 = f32[256,256]{1,0:T(8,128)} copy(f32[256,256]{1,0:T(8,128)S(1)} %get-tuple-element.7) | data formatting | bytes 524288

commit v4 on v3

--- a/solution.py
+++ b/solution.py
@@ -78,25 +78,28 @@
     other = pl.multiple_of((1 - core) * SIDE, SIDE)
 
     sign = 1 - 2 * core
-    bases = []
-    for step in range(16):
-        x_to = (x_pos + step % 4) % 4
-        place = ((y_pos + step // 4) % 4) * 16 + (x_to // 2) * 8
-        bases.append((x_to % 2, place, place + (x_to % 2) * 128 + core * 64))
+    z_places = [(z_pos + sign * dz + 8) % 8 for dz in (4, 3, 5, 2, 6, 1, 7, 0)]
+    x_places = []
+    for dx in (2, 3, 1, 0):
+        x_to = (x_pos + dx) % 4
+        high = (x_to // 2) * 8
+        x_places.append((x_to % 2, high, high + (x_to % 2) * 128 + core * 64))
 
     def each_peer(act):
-        def some(near, far, first):
-            for dz, start in ((near, 0), (far, first)):
-                z_to = (z_pos + sign * dz + 8) % 8
-                for x, place, device in bases[start:]:
-                    act(x, place + z_to, device + z_to)
+        def plane(dy, me_too):
+            y_place = ((y_pos + dy) % 4) * 16
+            places = [y_place + z_to for z_to in z_places]
+            for dx in range(4):
+                x, high, device = x_places[dx]
+                for place in places if dx < 3 or me_too else places[:7]:
+                    act(x, place + high, place + device)
 
         def several(step, carry):
-            some(4 - step, 5 + step, 0)
+            plane(3 - step, True)
             return carry
 
         lax.fori_loop(0, 3, several, 0)
-        some(1, 0, 1)
+        plane(0, False)
 
     def copy(source, landing, slot, device):
         return pltpu.make_async_remote_copy(
@@ -281,6 +284,17 @@
     swap_filter.wait()
     for half in range(2):
         out_filter[pl.ds(half * SIDE, SIDE), pl.ds(other, SIDE)] = pair_filter[pl.ds(half, SIDE, stride=2), :].T
+
+
+def put_out(input_near, filter_near, input_far, filter_far, sems):
+    copies = [
+        pltpu.make_async_copy(filter_near, filter_far, sems.at[0]),
+        pltpu.make_async_copy(input_near, input_far, sems.at[1]),
+    ]
+    for copy in copies:
+        copy.start()
+    for copy in copies:
+        copy.wait()
 
 
 def shards(signal, grad_out, filter_taps, skip_gain):
@@ -316,6 +330,17 @@
         ],
         compiler_params=pltpu.CompilerParams(collective_id=0, has_side_effects=True),
     )(signal[0], grad_out[0], filter_taps, skip_gain[None, :], *held)
+    place = pl.BlockSpec(memory_space=pl.ANY)
+    input_grad, filter_grad = pl.pallas_call(
+        put_out,
+        out_shape=(
+            jax.ShapeDtypeStruct((2 * SIDE, 2 * SIDE), BF16),
+            jax.ShapeDtypeStruct((2 * SIDE, 2 * SIDE), F32),
+        ),
+        in_specs=[vmem] * 2,
+        out_specs=(place, place),
+        scratch_shapes=[pltpu.SemaphoreType.DMA((2,))],
+    )(*(pltpu.with_memory_space_constraint(x, pltpu.VMEM) for x in (input_grad, filter_grad)))
     return input_grad[None], filter_grad
 
 

time: 44.1 us -> 42.6 us (0.966)
  local copies, waits for them, and re-layouts: 1.36 us -> 0 us
    unnamed x2 -> x0, local copies, waits for them, and re-layouts: 1.36 us -> none
    pallas_call x1, Pallas kernels: 42 us -> 41.1 us  [shards(): pl.pallas_call(body, out_shape=(pltpu.VMEM((2 * SIDE, 2 * SIDE), BF16), p...]
    pallas_call x0 -> x1, Pallas kernels: none -> 0.76 us  [shards(): pl.pallas_call(put_out, out_shape=(jax.ShapeDtypeStruct((2 * SIDE, 2 * SI...]
where the time goes in v4:
time: 42.6 us; the launch traced here: 42.5 us
  Pallas kernels  41.8 us (98%)
  between operations  0.64 us (2%)
    pallas_call x1, Pallas kernels, shards(): pl.pallas_call(body, out_shape=(pltpu.VMEM((2 * SIDE, 2 * SIDE), BF16), p...  41.1 us

profile of v4, /device:TPU:1, one launch (start us, length us, event | category | flops | bytes accessed | tf_op | source)
XLA Modules:
  0.0 42.5 jit_solution(11007384727097921369)
XLA Ops:
  0.6 41.1 %shard_map.104 = (bf16[256,256]{1,0:T(8,128)(2,1)S(1)}, f32[256,256]{1,0:T(8,128)S(1)}) custom-call(bf16[256,256]{1,0:T(8,128)(2,1)} %bitcast.4, bf16[256,256]{1,0:T(8,128)(2,1)} %bitcast.5, f32[256,256]{1,0:T(8,128)} %taps_far.1, f32[1,256]{1,0:T(1,128)} %bitcast.6, bf16[256,384]{1,0:T(8,128)(2,1)} %constant.10.clone.rest_0_, ...), custom_call_target="tpu_custom_call" | custom-call | tf_op jit(solution)/shard_map/pallas_call | solution.py:304
  41.7 0.8 %shard_map.105 = (bf16[256,256]{1,0:T(8,128)(2,1)}, f32[256,256]{1,0:T(8,128)}) custom-call(bf16[256,256]{1,0:T(8,128)(2,1)S(1)} %get-tuple-element.6.input_near, f32[256,256]{1,0:T(8,128)S(1)} %get-tuple-element.7.filter_near), custom_call_target="tpu_custom_call" | custom-call | tf_op jit(solution)/shard_map/pallas_call | solution.py:334

commit v5 on v4

--- a/solution.py
+++ b/solution.py
@@ -14,6 +14,12 @@
 LEN = SIDE * SIDE
 LOGICAL = pl.DeviceIdType.LOGICAL
 TAPS, GRAD, SIGNAL, INPUT, FILTER, SWAP_GRAD, SWAP_SIGNAL, SWAP_INPUT, SWAP_FILTER = range(9)
+
+
+ORDER = sorted(
+    [(dx, dy, dz) for dz in range(8) for dy in range(4) for dx in range(4) if dx + dy + dz],
+    key=lambda d: (-sum(min(step, size - step) for step, size in zip(d, (4, 4, 8))), min(d[2], 8 - d[2])),
+)
 
 
 def split_table(table):
@@ -78,28 +84,19 @@
     other = pl.multiple_of((1 - core) * SIDE, SIDE)
 
     sign = 1 - 2 * core
-    z_places = [(z_pos + sign * dz + 8) % 8 for dz in (4, 3, 5, 2, 6, 1, 7, 0)]
+    z_places = [(z_pos + sign * dz + 8) % 8 for dz in range(8)]
+    y_places = [((y_pos + dy) % 4) * 16 for dy in range(4)]
     x_places = []
-    for dx in (2, 3, 1, 0):
+    for dx in range(4):
         x_to = (x_pos + dx) % 4
         high = (x_to // 2) * 8
         x_places.append((x_to % 2, high, high + (x_to % 2) * 128 + core * 64))
 
     def each_peer(act):
-        def plane(dy, me_too):
-            y_place = ((y_pos + dy) % 4) * 16
-            places = [y_place + z_to for z_to in z_places]
-            for dx in range(4):
-                x, high, device = x_places[dx]
-                for place in places if dx < 3 or me_too else places[:7]:
-                    act(x, place + high, place + device)
-
-        def several(step, carry):
-            plane(3 - step, True)
-            return carry
-
-        lax.fori_loop(0, 3, several, 0)
-        plane(0, False)
+        for dx, dy, dz in ORDER:
+            place = y_places[dy] + z_places[dz]
+            x, high, device = x_places[dx]
+            act(x, place + high, place + device)
 
     def copy(source, landing, slot, device):
         return pltpu.make_async_remote_copy(

time: 42.6 us -> 42 us (0.986)
  Pallas kernels: 41.8 us -> 41.3 us
    pallas_call x1, Pallas kernels: 41.1 us -> 40.5 us  [shards(): pl.pallas_call(body, out_shape=(pltpu.VMEM((2 * SIDE, 2 * SIDE), BF16), p...]
where the time goes in v5:
time: 42 us; the launch traced here: 41.9 us
  Pallas kernels  41.3 us (98%)
  between operations  0.64 us (2%)
    pallas_call x1, Pallas kernels, shards(): pl.pallas_call(body, out_shape=(pltpu.VMEM((2 * SIDE, 2 * SIDE), BF16), p...  40.5 us

profile of v5, /device:TPU:1, one launch (start us, length us, event | category | flops | bytes accessed | tf_op | source)
XLA Modules:
  0.0 41.9 jit_solution(13666687753940118731)
XLA Ops:
  0.6 40.5 %shard_map.104 = (bf16[256,256]{1,0:T(8,128)(2,1)S(1)}, f32[256,256]{1,0:T(8,128)S(1)}) custom-call(bf16[256,256]{1,0:T(8,128)(2,1)} %bitcast.4, bf16[256,256]{1,0:T(8,128)(2,1)} %bitcast.5, f32[256,256]{1,0:T(8,128)} %taps_far.1, f32[1,256]{1,0:T(1,128)} %bitcast.6, bf16[256,384]{1,0:T(8,128)(2,1)} %constant.10.clone.rest_0_, ...), custom_call_target="tpu_custom_call" | custom-call | tf_op jit(solution)/shard_map/pallas_call | solution.py:301
  41.1 0.8 %shard_map.105 = (bf16[256,256]{1,0:T(8,128)(2,1)}, f32[256,256]{1,0:T(8,128)}) custom-call(bf16[256,256]{1,0:T(8,128)(2,1)S(1)} %get-tuple-element.6.input_near, f32[256,256]{1,0:T(8,128)S(1)} %get-tuple-element.7.filter_near), custom_call_target="tpu_custom_call" | custom-call | tf_op jit(solution)/shard_map/pallas_call | solution.py:331

commit v6 on v5

--- a/solution.py
+++ b/solution.py
@@ -144,7 +144,6 @@
     swap_grad = copy(stage_grad, send_grad.at[core], SWAP_GRAD, partner)
     swap_signal = copy(stage_signal, send_signal.at[core], SWAP_SIGNAL, partner)
     swap_grad.start()
-    swap_signal.start()
 
     taps_at = land_taps.at[pl.ds(2 * seq + x_low, 1)]
     send_all(lambda x, s: send_taps.at[pl.ds(64 * x + s, 1)], taps_at, TAPS)
@@ -155,6 +154,8 @@
         (swap_signal, send_signal, land_signal, SIGNAL),
     ):
         swap.wait()
+        if slot == GRAD:
+            swap_signal.start()
         send_all(
             lambda x, s, send=send: send.at[:, pl.ds(128 * x + 2 * s, 2), :],
             land.at[pl.ds(2 * x_low, 2), pl.ds(2 * seq, 2), :],

time: 42 us -> 41.9 us (level)
  no operation moved by 1% of the time
where the time goes in v6:
time: 41.9 us; the launch traced here: 41.8 us
  Pallas kernels  41.2 us (98%)
  between operations  0.64 us (2%)
    pallas_call x1, Pallas kernels, shards(): pl.pallas_call(body, out_shape=(pltpu.VMEM((2 * SIDE, 2 * SIDE), BF16), p...  40.4 us

profile of v6, /device:TPU:1, one launch (start us, length us, event | category | flops | bytes accessed | tf_op | source)
XLA Modules:
  0.0 41.8 jit_solution(14327079353388007858)
XLA Ops:
  0.6 40.4 %shard_map.104 = (bf16[256,256]{1,0:T(8,128)(2,1)S(1)}, f32[256,256]{1,0:T(8,128)S(1)}) custom-call(bf16[256,256]{1,0:T(8,128)(2,1)} %bitcast.4, bf16[256,256]{1,0:T(8,128)(2,1)} %bitcast.5, f32[256,256]{1,0:T(8,128)} %taps_far.1, f32[1,256]{1,0:T(1,128)} %bitcast.6, bf16[256,384]{1,0:T(8,128)(2,1)} %constant.10.clone.rest_0_, ...), custom_call_target="tpu_custom_call" | custom-call | tf_op jit(solution)/shard_map/pallas_call | solution.py:302
  41.1 0.8 %shard_map.105 = (bf16[256,256]{1,0:T(8,128)(2,1)}, f32[256,256]{1,0:T(8,128)}) custom-call(bf16[256,256]{1,0:T(8,128)(2,1)S(1)} %get-tuple-element.6.input_near, f32[256,256]{1,0:T(8,128)S(1)} %get-tuple-element.7.filter_near), custom_call_target="tpu_custom_call" | custom-call | tf_op jit(solution)/shard_map/pallas_call | solution.py:332

commit v7 on v6

--- a/solution.py
+++ b/solution.py
@@ -278,19 +278,25 @@
     swap_filter = copy(land_filter, pair_filter, SWAP_FILTER, partner)
     swap_filter.start()
     for half in range(2):
-        out_filter[pl.ds(half * SIDE, SIDE), pl.ds(own, SIDE)] = land_filter[pl.ds(half, SIDE, stride=2), :].T
+        out_filter[1, pl.ds(half * SIDE, SIDE), :] = land_filter[pl.ds(half, SIDE, stride=2), :].T
     swap_filter.wait()
+    out_filter[0] = pair_filter[...]
+
+
+def put_out(input_near, filter_near, input_far, filter_far, turned, sems):
+    core = lax.axis_index("batch") % 2
+    own = filter_far.at[:, pl.ds(pl.multiple_of(core * SIDE, SIDE), SIDE)]
+    other = filter_far.at[:, pl.ds(pl.multiple_of((1 - core) * SIDE, SIDE), SIDE)]
+    copies = [
+        pltpu.make_async_copy(filter_near.at[1], own, sems.at[0]),
+        pltpu.make_async_copy(input_near, input_far, sems.at[1]),
+        pltpu.make_async_copy(turned, other, sems.at[2]),
+    ]
+    copies[0].start()
+    copies[1].start()
     for half in range(2):
-        out_filter[pl.ds(half * SIDE, SIDE), pl.ds(other, SIDE)] = pair_filter[pl.ds(half, SIDE, stride=2), :].T
-
-
-def put_out(input_near, filter_near, input_far, filter_far, sems):
-    copies = [
-        pltpu.make_async_copy(filter_near, filter_far, sems.at[0]),
-        pltpu.make_async_copy(input_near, input_far, sems.at[1]),
-    ]
-    for copy in copies:
-        copy.start()
+        turned[pl.ds(half * SIDE, SIDE), :] = filter_near[0, pl.ds(half, SIDE, stride=2), :].T
+    copies[2].start()
     for copy in copies:
         copy.wait()
 
@@ -303,7 +309,7 @@
         body,
         out_shape=(
             pltpu.VMEM((2 * SIDE, 2 * SIDE), BF16),
-            pltpu.VMEM((2 * SIDE, 2 * SIDE), F32),
+            rows(2, 2 * SIDE),
         ),
         in_specs=[pl.BlockSpec(memory_space=pl.ANY)] * 9,
         out_specs=(vmem, vmem),
@@ -337,7 +343,7 @@
         ),
         in_specs=[vmem] * 2,
         out_specs=(place, place),
-        scratch_shapes=[pltpu.SemaphoreType.DMA((2,))],
+        scratch_shapes=[rows(2 * SIDE), pltpu.SemaphoreType.DMA((3,))],
     )(*(pltpu.with_memory_space_constraint(x, pltpu.VMEM) for x in (input_grad, filter_grad)))
     return input_grad[None], filter_grad
 

time: 41.9 us -> 41.9 us (level)
  no operation moved by 1% of the time
where the time goes in v7:
time: 41.9 us; the launch traced here: 41.8 us
  Pallas kernels  41.1 us (98%)
  between operations  0.64 us (2%)
    pallas_call x1, Pallas kernels, shards(): pl.pallas_call(body, out_shape=(pltpu.VMEM((2 * SIDE, 2 * SIDE), BF16), r...  40.4 us

profile of v7, /device:TPU:1, one launch (start us, length us, event | category | flops | bytes accessed | tf_op | source)
XLA Modules:
  0.0 41.8 jit_solution(17240541081630104079)
XLA Ops:
  0.6 40.4 %shard_map.104 = (bf16[256,256]{1,0:T(8,128)(2,1)S(1)}, f32[2,256,128]{2,1,0:T(8,128)S(1)}) custom-call(bf16[256,256]{1,0:T(8,128)(2,1)} %bitcast.4, bf16[256,256]{1,0:T(8,128)(2,1)} %bitcast.5, f32[256,256]{1,0:T(8,128)} %taps_far.1, f32[1,256]{1,0:T(1,128)} %bitcast.6, bf16[256,384]{1,0:T(8,128)(2,1)} %constant.10.clone.rest_0_, ...), custom_call_target="tpu_custom_call" | custom-call | tf_op jit(solution)/shard_map/pallas_call | solution.py:308
  41.0 0.8 %shard_map.105 = (bf16[256,256]{1,0:T(8,128)(2,1)}, f32[256,256]{1,0:T(8,128)}) custom-call(bf16[256,256]{1,0:T(8,128)(2,1)S(1)} %get-tuple-element.6.input_near, f32[2,256,128]{2,1,0:T(8,128)S(1)} %get-tuple-element.7.filter_near), custom_call_target="tpu_custom_call" | custom-call | tf_op jit(solution)/shard_map/pallas_call | solution.py:338
